TPU v7x, 32 devices: a whole 2x2x4 slice. The times are simulated.
32 devices in a mesh: rows: 8 (over y, x, core), grp: 4 (over z).
Axes of the slice: x: 2, y: 2, z: 4, core: 2. Of those that a mesh axis runs over, the one named last changes fastest.
Arguments:
- pivot_columns: bfloat16 [32, 10240, 256], P('rows', 'grp'), may hold values from -6 to 6
- previous: bfloat16 [32, 10240, 512], P('rows', 'grp'), may hold values from -0.59765625 to 0.59765625
- pivots: int32 [256], replicated, may hold values from 0 to 327679, as said below
- pivot_inverse: bfloat16 [256, 256], replicated, may hold values from -0.4 to 1.5
- orbitals: bfloat16 [10240, 1024], P('grp'), may hold values from -0.0625 to 0.0625
- slab_orbitals: bfloat16 [32, 1024], replicated, may hold values from -1 to 1
Outputs:
- new_vectors: bfloat16 [32, 10240, 256], P('rows', 'grp')
- mo_block: bfloat16 [256, 1024, 1024], P('rows', None, 'grp')
Inputs may be any that keep to these rules, and one draw needn't show every extreme that they name: `pivots`: distinct entries.
All inputs are finite; a program needn't handle non-finite values.
Results may differ from a plain program's by a relative error of at most 0.0038.
The roundings to bfloat16 on the way count: a program that leaves them out, or rounds other values in their place, can miss the bound.
Values may be sent and summed in bfloat16 or wider, within the bound.
A program may use at most 128 MiB of HBM per device.

v0:
```python
import jax
import jax.numpy as jnp
from jax import lax
from jax.sharding import PartitionSpec as P

NBAS = 10240


def per_device(pivot_columns, previous, pivots, pivot_inverse, orbitals, slab_orbitals):
    mu_dev, nu_dev, prev_count = previous.shape
    pivot_count = pivot_columns.shape[2]
    row_index = lax.axis_index("rows")
    grp_index = lax.axis_index("grp")
    first_local = pivots // NBAS - row_index * mu_dev
    second_local = pivots % NBAS - grp_index * nu_dev
    owned = (
        (first_local >= 0) & (first_local < mu_dev) & (second_local >= 0) & (second_local < nu_dev)
    )
    local_row = jnp.where(owned, first_local * nu_dev + second_local, 0)
    flat_prev = previous.reshape(mu_dev * nu_dev, prev_count)
    picked = jnp.where(
        owned[:, None], jnp.take(flat_prev, local_row, axis=0).astype(jnp.float32), 0.0
    )
    pivot_rows = lax.psum(picked, ("rows", "grp")).astype(jnp.bfloat16)
    correction = jnp.dot(flat_prev, pivot_rows.T, preferred_element_type=jnp.float32)
    flat_columns = pivot_columns.reshape(mu_dev * nu_dev, pivot_count)
    residual_columns = (flat_columns.astype(jnp.float32) - correction).astype(jnp.bfloat16)
    upper = jnp.triu(pivot_inverse)
    new_flat = jnp.dot(residual_columns, upper, preferred_element_type=jnp.float32).astype(
        jnp.bfloat16
    )
    new_vectors = new_flat.reshape(mu_dev, nu_dev, pivot_count)
    half = lax.psum_scatter(
        jnp.einsum("nj,mnp->jmp", orbitals, new_vectors, preferred_element_type=jnp.float32),
        "grp",
        scatter_dimension=0,
        tiled=True,
    ).astype(jnp.bfloat16)
    summed = jnp.einsum(
        "mi,jmp->pij",
        slab_orbitals,
        lax.all_to_all(half, "rows", split_axis=2, concat_axis=1, tiled=True),
        preferred_element_type=jnp.float32,
    )
    mo_block = summed.astype(jnp.bfloat16)
    return (new_vectors, mo_block)


def solution(mesh):
    in_specs = (P("rows", "grp", None), P("rows", "grp", None), P(), P(), P("grp", None), P())
    out_specs = (P("rows", "grp", None), P("rows", None, "grp"))
    return jax.shard_map(
        per_device, mesh=mesh, in_specs=in_specs, out_specs=out_specs, check_vma=False
    )
```

profile of v0, /device:TPU:0, one launch (start us, length us, event | category | flops | bytes accessed | tf_op | source)
XLA Modules:
  0.0 210.1 jit_solution(867711834112606244)
XLA Ops:
  7.2 0.0 copy-start
  7.2 0.0 reduce-scatter.2.cloned.1.call-start
  7.2 0.7 compare_and_fusion
  8.0 6.5 %gather_fusion = bf16[256,512]{1,0:T(8,128)(2,1)S(1)} fusion(bf16[10240,512]{1,0:T(8,128)(2,1)} %bitcast.36, s32[1024]{0:T(1024)S(1)} %pad_clamp_fusion), kind=kCustom, calls=%fused_computation | custom fusion | bytes 525312 | tf_op jit(solution)/shard_map/jit(_take)/gather | solution.py:22
  14.5 0.1 convert_select_fusion
  14.7 47.2 %all-reduce.1 = bf16[256,512]{1,0:T(8,128)(2,1)S(1)} all-reduce(f32[256,512]{1,0:T(8,128)S(1)} %convert_select_fusion), channel_id=1, replica_groups=mesh['rows'=8,'grp'=4] {'rows','grp'}, use_global_device_ids=true, to_apply=%region_0.1 | all-reduce | flops 131072 | bytes 786432 | tf_op jit(solution)/shard_map/psum | solution.py:24
  61.9 9.6 %convolution_convert_fusion = bf16[10240,256]{1,0:T(8,128)(2,1)} fusion(bf16[10240,512]{1,0:T(8,128)(2,1)} %bitcast.37, bf16[10240,256]{1,0:T(8,128)(2,1)} %bitcast.38, bf16[256,512]{1,0:T(8,128)(2,1)S(1)} %all-reduce.1, bf16[256,256]{1,0:T(8,128)(2,1)} %param.9, s32[256]{0:T(256)S(1)} %iota_add_fusion), kind=kOutput, calls=%fused_computation.5 | convolution fusion | flops 4037148672 | bytes 21365760 | tf_op jit(solution)/shard_map/dot_general | solution.py:29
  71.5 10.4 %fusion.4 = f32[1024,4,256]{0,2,1:T(8,128)} fusion(bf16[4,2560,256]{2,1,0:T(8,128)(2,1)} %bitcast.39, bf16[2560,1024]{1,0:T(8,128)(2,1)} %param.10), kind=kOutput, calls=%fused_computation.8 | convolution fusion | flops 5368709120 | bytes 14680064 | tf_op jit(solution)/shard_map/nj,mnp->jmp/dot_general | solution.py:34
  81.9 0.0 reduce-scatter.2.cloned.1.call-update
  81.9 75.4 %reduce-scatter.2.cloned.1.call-done = f32[256,4,256]{0,2,1:T(8,128)} async-done(((f32[1024,4,256]{0,2,1:T(8,128)}), f32[256,4,256]{0,2,1:T(8,128)}) %reduce-scatter.2.cloned.1.call-update) | async-done | bytes 1048592 | tf_op jit(solution)/shard_map/reduce_scatter | solution.py:33
  157.3 1.3 convert_element_type.33
  158.6 0.4 copy.12
  159.0 13.2 %all_to_all.18 = bf16[256,4,256]{0,1,2:T(4,128)(2,1)S(1)} all-to-all(bf16[256,4,256]{0,1,2:T(4,128)(2,1)S(1)} %copy.12), channel_id=1, replica_groups=mesh['rows'=8,'grp'=4] {'rows'}, dimensions={2} | all-to-all | bytes 1048576 | tf_op jit(solution)/shard_map/all_to_all | solution.py:42
  172.2 0.3 copy.17
  172.5 0.1 all_to_all.16
  172.6 0.0 copy-done
  172.6 8.1 %convert_bitcast_fusion = bf16[32,1024,256]{1,2,0:T(8,128)(2,1)} fusion(bf16[256,32,32]{0,1,2:T(8,128)(2,1)S(1)} %all_to_all.16, bf16[32,1024]{1,0:T(8,128)(2,1)S(1)} %copy-done), kind=kOutput, calls=%fused_computation.1 | convolution fusion | flops 545259520 | bytes 17367040 | tf_op jit(solution)/shard_map/mi,jmp->pij/dot_general | solution.py:39
  180.8 0.0 copy-start.1
  180.8 22.5 %copy.14 = bf16[32,1024,256]{2,1,0:T(8,128)(2,1)} copy(bf16[32,1024,256]{1,2,0:T(8,128)(2,1)} %convert_bitcast_fusion) | data formatting | bytes 33554432
  203.2 0.0 copy-done.1
  (2 shorter events, 0.0 us)
Async XLA Ops:
  7.2 165.5 %copy-start = (bf16[32,1024]{1,0:T(8,128)(2,1)S(1)}, bf16[32,1024]{1,0:T(8,128)(2,1)}, u32[]{:S(2)}) copy-start(bf16[32,1024]{1,0:T(8,128)(2,1)} %param.11) | copy-start | bytes 196612
  7.2 150.1 %reduce-scatter.2.cloned.1.call-start = ((), (), s32[]{:S(2)}) async-start(), calls=%async_computation.2 | async-start | bytes 5242880 | tf_op jit(solution)/shard_map/reduce_scatter | solution.py:33
  180.8 22.5 %copy-start.1 = (bf16[32,1024]{1,0:T(8,128)(2,1)S(1)}, bf16[32,1024]{1,0:T(8,128)(2,1)}, u32[]{:S(2)}) copy-start(bf16[32,1024]{1,0:T(8,128)(2,1)} %param.11) | copy-start | bytes 196612
Sparse Core Ops, SparseCore 0:
  82.0 75.2 reduce-scatter.1
where the time goes:
time: 211 us; the launch traced here: 210 us
  waiting for transfers between devices  75.4 us (36%)
  blocking collectives  60.4 us (29%)
  local copies, waits for them, and re-layouts  29.8 us (14%)
  matrix products  28.1 us (13%)
  between operations  14.1 us (7%)
  other arithmetic  2.13 us (1%)
    reduce_scatter x1, waiting for transfers between devices, per_device(): lax.psum_scatter(jnp.einsum('nj,mnp->jmp', orbitals, new_vectors, preferr...  75.4 us
    psum x1, blocking collectives, per_device(): pivot_rows = lax.psum(picked, ('rows', 'grp')).astype(jnp.bfloat16)  47.2 us
    unnamed x5, local copies, waits for them, and re-layouts  22.5 us
    all_to_all x1, blocking collectives, per_device(): lax.all_to_all(half, 'rows', split_axis=2, concat_axis=1, tiled=True)  13.2 us
    dot_general x1, matrix products, per_device(): jnp.einsum('nj,mnp->jmp', orbitals, new_vectors, preferred_element_type=j...  10.4 us
    dot_general x1, matrix products, per_device(): jnp.dot(residual_columns, upper, preferred_element_type=jnp.float32)  9.58 us
    dot_general x1, matrix products, per_device(): jnp.einsum('mi,jmp->pij', slab_orbitals, lax.all_to_all(half, 'rows', spl...  8.14 us
    gather x1, local copies, waits for them, and re-layouts, per_device(): jnp.take(flat_prev, local_row, axis=0).astype(jnp.float32)  6.54 us
  transfers between devices with their start and end apart: 1, of which 1 were waited for; matrix products, arithmetic and copies ran while one was open for 0% of the time, Pallas kernels for 0%

commit v1 on v0

--- a/solution.py
+++ b/solution.py
@@ -21,7 +21,7 @@
     picked = jnp.where(
         owned[:, None], jnp.take(flat_prev, local_row, axis=0).astype(jnp.float32), 0.0
     )
-    pivot_rows = lax.psum(picked, ("rows", "grp")).astype(jnp.bfloat16)
+    pivot_rows = lax.psum(lax.psum(picked, "grp"), "rows").astype(jnp.bfloat16)
     correction = jnp.dot(flat_prev, pivot_rows.T, preferred_element_type=jnp.float32)
     flat_columns = pivot_columns.reshape(mu_dev * nu_dev, pivot_count)
     residual_columns = (flat_columns.astype(jnp.float32) - correction).astype(jnp.bfloat16)

time: 211 us -> 236 us (1.12)
  waiting for transfers between devices: 75.4 us -> 116 us
  blocking collectives: 60.4 us -> 44.1 us
    psum x0 -> x1, waiting for transfers between devices: none -> 41.3 us  [per_device(): pivot_rows = lax.psum(lax.psum(picked, 'grp'), 'rows').astype(jnp.bfloat16)]
    psum x1, blocking collectives: 47.2 us -> 30.9 us  [per_device(): pivot_rows = lax.psum(lax.psum(picked, 'grp'), 'rows').astype(jnp.bfloat16)]
  transfers between devices with their start and end apart: 1 -> 2, of which waited for: 1 -> 2; matrix products, arithmetic and copies ran while one was open for 0% -> 0% of each run, Pallas kernels for 0% -> 0%
where the time goes in v1:
time: 236 us; the launch traced here: 235 us
  waiting for transfers between devices  116 us (49%)
  blocking collectives  44.1 us (19%)
  local copies, waits for them, and re-layouts  29.8 us (13%)
  matrix products  28.1 us (12%)
  between operations  14.1 us (6%)
  other arithmetic  2.92 us (1%)
    reduce_scatter x1, waiting for transfers between devices, per_device(): lax.psum_scatter(jnp.einsum('nj,mnp->jmp', orbitals, new_vectors, preferr...  74.3 us
    psum x1, waiting for transfers between devices, per_device(): pivot_rows = lax.psum(lax.psum(picked, 'grp'), 'rows').astype(jnp.bfloat16)  41.3 us
    psum x1, blocking collectives, per_device(): pivot_rows = lax.psum(lax.psum(picked, 'grp'), 'rows').astype(jnp.bfloat16)  30.9 us
    unnamed x5, local copies, waits for them, and re-layouts  22.5 us
    all_to_all x1, blocking collectives, per_device(): lax.all_to_all(half, 'rows', split_axis=2, concat_axis=1, tiled=True)  13.2 us
    dot_general x1, matrix products, per_device(): jnp.einsum('nj,mnp->jmp', orbitals, new_vectors, preferred_element_type=j...  10.4 us
    dot_general x1, matrix products, per_device(): jnp.dot(residual_columns, upper, preferred_element_type=jnp.float32)  9.56 us
    dot_general x1, matrix products, per_device(): jnp.einsum('mi,jmp->pij', slab_orbitals, lax.all_to_all(half, 'rows', spl...  8.14 us
  transfers between devices with their start and end apart: 2, of which 2 were waited for; matrix products, arithmetic and copies ran while one was open for 0% of the time, Pallas kernels for 0%

profile of v1, /device:TPU:0, one launch (start us, length us, event | category | flops | bytes accessed | tf_op | source)
XLA Modules:
  0.0 234.8 jit_solution(2680704401957630629)
XLA Ops:
  7.2 0.0 copy-start
  7.2 0.0 all-reduce.3.cloned.1.call-start
  7.2 0.7 compare_and_fusion
  8.0 6.5 %gather_fusion = bf16[256,512]{1,0:T(8,128)(2,1)S(1)} fusion(bf16[10240,512]{1,0:T(8,128)(2,1)} %bitcast.36, s32[1024]{0:T(1024)S(1)} %pad_clamp_fusion), kind=kCustom, calls=%fused_computation | custom fusion | bytes 525312 | tf_op jit(solution)/shard_map/jit(_take)/gather | solution.py:22
  14.5 0.9 convert_select_fusion
  15.4 0.0 all-reduce.3.cloned.1.call-update
  15.5 0.0 reduce-scatter.2.cloned.1.call-start
  15.5 41.3 %all-reduce.3.cloned.1.call-done = f32[256,512]{1,0:T(8,128)} async-done(((f32[256,512]{1,0:T(8,128)}), f32[256,512]{1,0:T(8,128)}) %all-reduce.3.cloned.1.call-update) | async-done | bytes 524304 | tf_op jit(solution)/shard_map/psum | solution.py:24
  56.8 30.9 %all-reduce.4 = bf16[256,512]{1,0:T(8,128)(2,1)S(1)} all-reduce(f32[256,512]{1,0:T(8,128)} %all-reduce.3.cloned.1.call-done), channel_id=1, replica_groups=mesh['rows'=8,'grp'=4] {'rows'}, use_global_device_ids=true, to_apply=%region_1.2 | all-reduce | flops 131072 | bytes 786432 | tf_op jit(solution)/shard_map/psum | solution.py:24
  87.8 9.6 %convolution_convert_fusion = bf16[10240,256]{1,0:T(8,128)(2,1)} fusion(bf16[10240,512]{1,0:T(8,128)(2,1)} %bitcast.37, bf16[10240,256]{1,0:T(8,128)(2,1)} %bitcast.38, bf16[256,512]{1,0:T(8,128)(2,1)S(1)} %all-reduce.4, bf16[256,256]{1,0:T(8,128)(2,1)} %param.9, s32[256]{0:T(256)S(1)} %iota_add_fusion), kind=kOutput, calls=%fused_computation.5 | convolution fusion | flops 4037148672 | bytes 21365760 | tf_op jit(solution)/shard_map/dot_general | solution.py:29
  97.4 10.4 %fusion.4 = f32[1024,4,256]{0,2,1:T(8,128)} fusion(bf16[4,2560,256]{2,1,0:T(8,128)(2,1)} %bitcast.39, bf16[2560,1024]{1,0:T(8,128)(2,1)} %param.10), kind=kOutput, calls=%fused_computation.8 | convolution fusion | flops 5368709120 | bytes 14680064 | tf_op jit(solution)/shard_map/nj,mnp->jmp/dot_general | solution.py:34
  107.8 0.0 reduce-scatter.2.cloned.1.call-update
  107.8 74.3 %reduce-scatter.2.cloned.1.call-done = f32[256,4,256]{0,2,1:T(8,128)} async-done(((f32[1024,4,256]{0,2,1:T(8,128)}), f32[256,4,256]{0,2,1:T(8,128)}) %reduce-scatter.2.cloned.1.call-update) | async-done | bytes 1048592 | tf_op jit(solution)/shard_map/reduce_scatter | solution.py:33
  182.1 1.3 convert_element_type.33
  183.4 0.4 copy.12
  183.8 13.2 %all_to_all.18 = bf16[256,4,256]{0,1,2:T(4,128)(2,1)S(1)} all-to-all(bf16[256,4,256]{0,1,2:T(4,128)(2,1)S(1)} %copy.12), channel_id=1, replica_groups=mesh['rows'=8,'grp'=4] {'rows'}, dimensions={2} | all-to-all | bytes 1048576 | tf_op jit(solution)/shard_map/all_to_all | solution.py:42
  197.0 0.3 copy.17
  197.3 0.1 all_to_all.16
  197.4 0.0 copy-done
  197.4 8.1 %convert_bitcast_fusion = bf16[32,1024,256]{1,2,0:T(8,128)(2,1)} fusion(bf16[256,32,32]{0,1,2:T(8,128)(2,1)S(1)} %all_to_all.16, bf16[32,1024]{1,0:T(8,128)(2,1)S(1)} %copy-done), kind=kOutput, calls=%fused_computation.1 | convolution fusion | flops 545259520 | bytes 17367040 | tf_op jit(solution)/shard_map/mi,jmp->pij/dot_general | solution.py:39
  205.5 0.0 copy-start.1
  205.5 22.5 %copy.14 = bf16[32,1024,256]{2,1,0:T(8,128)(2,1)} copy(bf16[32,1024,256]{1,2,0:T(8,128)(2,1)} %convert_bitcast_fusion) | data formatting | bytes 33554432
  228.0 0.0 copy-done.1
  (2 shorter events, 0.0 us)
Async XLA Ops:
  7.2 190.2 %copy-start = (bf16[32,1024]{1,0:T(8,128)(2,1)S(1)}, bf16[32,1024]{1,0:T(8,128)(2,1)}, u32[]{:S(2)}) copy-start(bf16[32,1024]{1,0:T(8,128)(2,1)} %param.11) | copy-start | bytes 196612
  7.2 49.7 %all-reduce.3.cloned.1.call-start = ((), (), s32[]{:S(2)}) async-start(), calls=%async_computation.2 | async-start | bytes 1048576 | tf_op jit(solution)/shard_map/psum | solution.py:24
  15.5 166.7 %reduce-scatter.2.cloned.1.call-start = ((), (), s32[]{:S(2)}) async-start(), calls=%async_computation.3 | async-start | bytes 5242880 | tf_op jit(solution)/shard_map/reduce_scatter | solution.py:33
  205.5 22.5 %copy-start.1 = (bf16[32,1024]{1,0:T(8,128)(2,1)S(1)}, bf16[32,1024]{1,0:T(8,128)(2,1)}, u32[]{:S(2)}) copy-start(bf16[32,1024]{1,0:T(8,128)(2,1)} %param.11) | copy-start | bytes 196612
Sparse Core Ops, SparseCore 0:
  15.6 41.2 all-reduce.2
  107.9 74.1 reduce-scatter.1
